TPU v7x, 32 devices: a whole 2x2x4 slice. The times are simulated.
32 devices in a mesh: dom: 8 (over z, y), level: 4 (over x, core).
Axes of the slice: x: 2, y: 2, z: 4, core: 2. Of those that a mesh axis runs over, the one named last changes fastest.
Arguments:
- dg_values: bfloat16 [98304, 384], P(('dom', 'level')), may hold values from -6 to 6
- stiff_mu: bfloat16 [384, 384], replicated, may hold values from -0.1 to 2, as said below
- stiff_lam: bfloat16 [384, 384], replicated, may hold values from -0.1 to 2, as said below
- coef_mu: float32 [98304], P(('dom', 'level')), may hold values from 0.25 to 4
- coef_lam: float32 [98304], P(('dom', 'level')), may hold values from 0.25 to 4
- elem_count: int32 [32], P(('dom', 'level')), may hold values from 384 to 3072, as said below
- elem_block: int32 [3, 98304], P(None, ('dom', 'level')), may hold values from 0 to 1023
- share_map: int32 [32, 8, 32], P(('dom', 'level')), may hold values from 0 to 1024, as said below
- hang_child: int32 [32, 64], P(('dom', 'level')), may hold values from 0 to 1024, as said below
- hang_parent: int32 [32, 64, 2], P(('dom', 'level')), may hold values from 0 to 1023
Outputs:
- projected: float32 [3, 32768, 128], P(None, ('dom', 'level'))
- energy: float32 [], replicated
Inputs may be any that keep to these rules, and one draw needn't show every extreme that they name: `elem_count`: between 384 and 3072; one device, drawn anew, holds exactly 3072. `share_map`: Slots agree in pairs: [d, o, s] is live exactly when the partner's [d2, o', s] is live, and they name the same DoF block. Slots toward ranks outside 0 to 7 are empty. For every offset some rank pair fills all 32 slots. `hang_child`: on each device of level index 1 or more, 64 distinct blocks below 1024; on devices of level index 0 every entry is 1024 (no hanging blocks). `hang_parent`: block numbers on the device of the same rank and the next lower level index; unused on level index 0. `stiff_mu`: Symmetric. `stiff_lam`: Symmetric.
All inputs are finite; a program needn't handle non-finite values.
Results may differ from a plain program's by a relative error of at most 0.0003.
Values sent between devices are 32-bit elements; how exact they have to be, the bound alone decides.
A program may use at most 64 MiB of HBM per device.

v0:
```python
import jax
import jax.numpy as jnp
from jax import lax
from jax.sharding import PartitionSpec as P


def from_behind(block, axis, distance):
    devices = range(lax.axis_size(axis))
    route = [(i - distance, i) for i in devices if i - distance in devices]
    return lax.ppermute(block, axis, route)


def shards(
    dg_values,
    stiff_mu,
    stiff_lam,
    coef_mu,
    coef_lam,
    elem_count,
    elem_block,
    share_map,
    hang_child,
    hang_parent,
):
    elements = dg_values.shape[0]
    row_width = stiff_mu.shape[0]
    block_size = row_width // 3
    block_count = elements // 3
    offsets_half = share_map.shape[1] // 2
    joined = jnp.concatenate((stiff_mu, stiff_lam), axis=1)
    product = jnp.dot(dg_values, joined, preferred_element_type=jnp.float32)
    forces = coef_mu[:, None] * product[:, :row_width] + coef_lam[:, None] * product[:, row_width:]
    live_rows = jnp.arange(elements) < elem_count[0]
    forces = jnp.where(live_rows[:, None], forces, jnp.float32(0.0))
    energy_part = 0.5 * jnp.sum(dg_values.astype(jnp.float32) * forces)
    component_forces = jnp.transpose(forces.reshape(elements, 3, block_size), (1, 0, 2))
    block_ids = jnp.arange(block_count + 1, dtype=jnp.int32)

    def sum_blocks(packed):
        target_ids, component_part = packed
        selector = (block_ids[:, None] == target_ids[None, :]).astype(jnp.float32)
        return jnp.dot(
            selector,
            component_part,
            precision=lax.Precision.HIGHEST,
            preferred_element_type=jnp.float32,
        )

    local_blocks = lax.map(sum_blocks, (elem_block, component_forces))
    slot_blocks = share_map[0]
    outgoing = jnp.transpose(local_blocks[:, slot_blocks, :], (1, 0, 2, 3))
    offsets = [step + 1 for step in range(offsets_half)] + [
        -(step + 1) for step in range(offsets_half)
    ]
    pieces = [None] * (2 * offsets_half)
    for slot_index in range(2 * offsets_half):
        opposite = (slot_index + offsets_half) % (2 * offsets_half)
        pieces[opposite] = from_behind(outgoing[slot_index], "dom", offsets[slot_index])
    incoming = jnp.stack(pieces)
    received = jnp.transpose(incoming, (1, 0, 2, 3)).reshape(3, -1, block_size)
    assembled = local_blocks.at[:, slot_blocks.reshape(-1), :].add(received)
    wanted = from_behind(hang_parent, "level", -1)
    chosen = assembled[:, wanted[0].reshape(-1), :]
    picked = from_behind(chosen, "level", 1)
    parent_pairs = picked.reshape(3, -1, 2, block_size)
    child_values = 0.5 * (parent_pairs[:, :, 0] + parent_pairs[:, :, 1])
    projected = assembled.at[:, hang_child[0], :].set(child_values)
    scale_total = jnp.float32(row_width * elements * lax.axis_size("dom") * lax.axis_size("level"))
    energy = lax.psum(energy_part, ("dom", "level")) / scale_total
    return (projected[:, :block_count], energy)


def solution(mesh):
    return jax.shard_map(
        shards,
        mesh=mesh,
        in_specs=(
            P(("dom", "level"), None),
            P(),
            P(),
            P(("dom", "level")),
            P(("dom", "level")),
            P(("dom", "level")),
            P(None, ("dom", "level")),
            P(("dom", "level"), None, None),
            P(("dom", "level"), None),
            P(("dom", "level"), None, None),
        ),
        out_specs=(P(None, ("dom", "level"), None), P()),
        check_vma=False,
    )
```

profile of v0, /device:TPU:18, one launch (start us, length us, event | category | flops | bytes accessed | tf_op | source)
XLA Modules:
  0.0 186.4 jit_solution(15404276880878706162)
XLA Ops:
  0.6 1.9 %collective-permute-start.8 = (s32[1,64,2]{1,2,0:T(2,128)}, s32[1,64,2]{1,2,0:T(2,128)S(1)}, u32[]{:S(2)}, u32[]{:S(2)}) collective-permute-start(s32[1,64,2]{1,2,0:T(2,128)} %param.21), channel_id=1, source_target_pairs={{1,0},{2,1},{3,2},{5,4},{6,5},{7,6},{9,8},{10,9},{11,10},{13,12},{... | collective-permute-start | bytes 1544 | tf_op jit(solution)/shard_map/ppermute | solution.py:10
  2.6 4.4 %copy.33 = bf16[3072,384]{0,1:T(8,128)(2,1)} copy(bf16[3072,384]{1,0:T(8,128)(2,1)} %param.12) | data formatting | bytes 4718592 | tf_op args[0]
  7.8 2.7 %convolution_bitcast_fusion = f32[3072,768]{0,1:T(8,128)S(1)} fusion(bf16[3072,384]{1,0:T(8,128)(2,1)S(1)} %copy-done, bf16[384,384]{1,0:T(8,128)(2,1)S(1)} %copy-done.3, bf16[384,384]{1,0:T(8,128)(2,1)S(1)} %copy-done.4), kind=kOutput, calls=%fused_computation.13 | convolution fusion | flops 1813118976 | bytes 12386304 | tf_op jit(solution)/shard_map/dot_general | solution.py:31
  10.4 4.5 %multiply_reduce_fusion = (f32[]{:T(128)}, f32[3072,384]{0,1:T(8,128)}) fusion(bf16[3072,384]{0,1:T(8,128)(2,1)S(1)} %copy-done.1, f32[3072,768]{0,1:T(8,128)S(1)} %convolution_bitcast_fusion, f32[3072]{0:T(1024)S(1)} %copy-done.6, f32[3072]{0:T(1024)S(1)} %copy-done.7, pred[3072]{0:T(1024)(128)(4,1)S(1)} %iota_compare_fusion.4), kind=kLoop, calls=%fused_computation.18 | loop fusion | flops 8257535 | bytes 16542724 | tf_op jit(solution)/shard_map/reduce_sum | solution.py:35
  14.9 6.2 %copy.27 = f32[3072,3,128]{2,0,1:T(8,128)} copy(f32[3072,3,128]{0,2,1:T(8,128)} %bitcast.88) | data formatting | bytes 9437184 | tf_op jit(solution)/shard_map/reshape | solution.py:36
  21.1 73.7 %while.11 = (s32[]{:T(128)}, f32[3,1025,128]{2,0,1:T(4,128)S(1)}, s32[3,3072]{1,0:T(4,128)}, f32[3,3072,128]{2,1,0:T(8,128)}, s32[]{:T(128)}, /*index=5*/s32[]{:T(128)}) while((s32[]{:T(128)}, f32[3,1025,128]{2,0,1:T(4,128)S(1)}, s32[3,3072]{1,0:T(4,128)}, f32[3,3072,128]{2,1,0:T(8,128)}, s32[]{:T(128)}, /*index=5*/s32[]{:T(128)}) %tuple.40), condition=%wide.region_1.2_spmd.clone, body=%wide.region_0.1_spmd.clone.sunk | while | flops 4839705600 | bytes 4234317 | solution.py:49
  21.9 7.2 %fusion.24 = f32[1,1025,128]{2,1,0:T(8,128)S(1)} fusion(s32[3072]{0:T(1024)S(1)} %bitcast.92, f32[3,3072,128]{2,1,0:T(8,128)} %get-tuple-element.104, s32[]{:T(128)} %get-tuple-element.95), kind=kOutput, calls=%fused_computation.8.clone.1 | convolution fusion | flops 4839705600 | bytes 2110464 | tf_op jit(solution)/shard_map/while/body/eval_jaxpr/dot_general | solution.py:42
  29.1 3.3 %copy.41 = f32[1,1025,128]{2,0,1:T(1,128)S(1)} copy(f32[1,1025,128]{2,1,0:T(8,128)S(1)} %fusion.24) | data formatting | bytes 1049600 | tf_op jit(solution)/shard_map/while/body/jit(dynamic_update_index_in_dim)/dynamic_update_slice | solution.py:49
  32.4 13.2 %dynamic_update_slice.6 = f32[3,1025,128]{2,0,1:T(4,128)S(1)} dynamic-update-slice(f32[3,1025,128]{2,0,1:T(4,128)S(1)} %get-tuple-element.96, f32[1,1025,128]{2,0,1:T(1,128)S(1)} %copy.41, s32[]{:T(128)} %get-tuple-element.95, s32[]{:T(128)} %constant.11.clone.1..sunk, s32[]{:T(128)} %constant.11.clone.1..sunk) | dynamic-update-slice | bytes 1049604 | tf_op jit(solution)/shard_map/while/body/jit(dynamic_update_index_in_dim)/dynamic_update_slice | solution.py:49
  46.5 7.2 %fusion.24 = f32[1,1025,128]{2,1,0:T(8,128)S(1)} fusion(s32[3072]{0:T(1024)S(1)} %bitcast.92, f32[3,3072,128]{2,1,0:T(8,128)} %get-tuple-element.104, s32[]{:T(128)} %get-tuple-element.95), kind=kOutput, calls=%fused_computation.8.clone.1 | convolution fusion | flops 4839705600 | bytes 2110464 | tf_op jit(solution)/shard_map/while/body/eval_jaxpr/dot_general | solution.py:42
  53.7 3.3 %copy.41 = f32[1,1025,128]{2,0,1:T(1,128)S(1)} copy(f32[1,1025,128]{2,1,0:T(8,128)S(1)} %fusion.24) | data formatting | bytes 1049600 | tf_op jit(solution)/shard_map/while/body/jit(dynamic_update_index_in_dim)/dynamic_update_slice | solution.py:49
  57.0 13.2 %dynamic_update_slice.6 = f32[3,1025,128]{2,0,1:T(4,128)S(1)} dynamic-update-slice(f32[3,1025,128]{2,0,1:T(4,128)S(1)} %get-tuple-element.96, f32[1,1025,128]{2,0,1:T(1,128)S(1)} %copy.41, s32[]{:T(128)} %get-tuple-element.95, s32[]{:T(128)} %constant.11.clone.1..sunk, s32[]{:T(128)} %constant.11.clone.1..sunk) | dynamic-update-slice | bytes 1049604 | tf_op jit(solution)/shard_map/while/body/jit(dynamic_update_index_in_dim)/dynamic_update_slice | solution.py:49
  71.0 7.2 %fusion.24 = f32[1,1025,128]{2,1,0:T(8,128)S(1)} fusion(s32[3072]{0:T(1024)S(1)} %bitcast.92, f32[3,3072,128]{2,1,0:T(8,128)} %get-tuple-element.104, s32[]{:T(128)} %get-tuple-element.95), kind=kOutput, calls=%fused_computation.8.clone.1 | convolution fusion | flops 4839705600 | bytes 2110464 | tf_op jit(solution)/shard_map/while/body/eval_jaxpr/dot_general | solution.py:42
  78.2 3.3 %copy.41 = f32[1,1025,128]{2,0,1:T(1,128)S(1)} copy(f32[1,1025,128]{2,1,0:T(8,128)S(1)} %fusion.24) | data formatting | bytes 1049600 | tf_op jit(solution)/shard_map/while/body/jit(dynamic_update_index_in_dim)/dynamic_update_slice | solution.py:49
  81.5 13.2 %dynamic_update_slice.6 = f32[3,1025,128]{2,0,1:T(4,128)S(1)} dynamic-update-slice(f32[3,1025,128]{2,0,1:T(4,128)S(1)} %get-tuple-element.96, f32[1,1025,128]{2,0,1:T(1,128)S(1)} %copy.41, s32[]{:T(128)} %get-tuple-element.95, s32[]{:T(128)} %constant.11.clone.1..sunk, s32[]{:T(128)} %constant.11.clone.1..sunk) | dynamic-update-slice | bytes 1049604 | tf_op jit(solution)/shard_map/while/body/jit(dynamic_update_index_in_dim)/dynamic_update_slice | solution.py:49
  95.9 1.0 gather_fusion
  97.0 3.3 %collective-permute-start = (f32[3,32,128]{2,0,1:T(4,128)S(1)}, f32[3,32,128]{2,0,1:T(4,128)S(1)}, u32[]{:S(2)}, u32[]{:S(2)}) collective-permute-start(f32[3,32,128]{2,0,1:T(4,128)S(1)} %get-tuple-element.61), channel_id=1, source_target_pairs={{4,0},{8,4},{12,8},{16,12},{20,16},{24,20},{28,24},{5,1},{9,5},{13... | collective-permute-start | bytes 147464 | tf_op jit(solution)/shard_map/ppermute | solution.py:10
  100.3 40.1 %psum.7 = f32[]{:T(128)} all-reduce(f32[]{:T(128)S(6)} %mul.39), channel_id=1, replica_groups=mesh['dom'=8,'level'=4] {'dom','level'}, use_global_device_ids=true, to_apply=%region_5.6 | all-reduce | flops 1 | bytes 8 | tf_op jit(solution)/shard_map/psum | solution.py:69
  141.1 2.5 %collective-permute-start.1 = (f32[3,32,128]{2,0,1:T(4,128)S(1)}, f32[3,32,128]{2,0,1:T(4,128)S(1)}, u32[]{:S(2)}, u32[]{:S(2)}) collective-permute-start(f32[3,32,128]{2,0,1:T(4,128)S(1)} %get-tuple-element.60), channel_id=1, source_target_pairs={{8,0},{12,4},{16,8},{20,12},{24,16},{28,20},{9,1},{13,5},{17,9},{2... | collective-permute-start | bytes 147464 | tf_op jit(solution)/shard_map/ppermute | solution.py:10
  143.7 2.2 %collective-permute-start.2 = (f32[3,32,128]{2,0,1:T(4,128)S(1)}, f32[3,32,128]{2,0,1:T(4,128)S(1)}, u32[]{:S(2)}, u32[]{:S(2)}) collective-permute-start(f32[3,32,128]{2,0,1:T(4,128)S(1)} %get-tuple-element.59), channel_id=1, source_target_pairs={{12,0},{16,4},{20,8},{24,12},{28,16},{13,1},{17,5},{21,9},{25,13},... | collective-permute-start | bytes 147464 | tf_op jit(solution)/shard_map/ppermute | solution.py:10
  145.9 1.3 collective-permute-start.3
  147.2 3.6 %collective-permute-start.4 = (f32[3,32,128]{2,0,1:T(4,128)S(1)}, f32[3,32,128]{2,0,1:T(4,128)S(1)}, u32[]{:S(2)}, u32[]{:S(2)}) collective-permute-start(f32[3,32,128]{2,0,1:T(4,128)S(1)} %get-tuple-element.57), channel_id=1, source_target_pairs={{0,4},{4,8},{8,12},{12,16},{16,20},{20,24},{24,28},{1,5},{5,9},{9,... | collective-permute-start | bytes 147464 | tf_op jit(solution)/shard_map/ppermute | solution.py:10
  150.8 4.1 %collective-permute-start.5 = (f32[3,32,128]{2,0,1:T(4,128)S(1)}, f32[3,32,128]{2,0,1:T(4,128)S(1)}, u32[]{:S(2)}, u32[]{:S(2)}) collective-permute-start(f32[3,32,128]{2,0,1:T(4,128)S(1)} %get-tuple-element.56), channel_id=1, source_target_pairs={{0,8},{4,12},{8,16},{12,20},{16,24},{20,28},{1,9},{5,13},{9,17},{1... | collective-permute-start | bytes 147464 | tf_op jit(solution)/shard_map/ppermute | solution.py:10
  154.9 1.9 %collective-permute-start.6 = (f32[3,32,128]{2,0,1:T(4,128)S(1)}, f32[3,32,128]{2,0,1:T(4,128)S(1)}, u32[]{:S(2)}, u32[]{:S(2)}) collective-permute-start(f32[3,32,128]{2,0,1:T(4,128)S(1)} %get-tuple-element.55), channel_id=1, source_target_pairs={{0,12},{4,16},{8,20},{12,24},{16,28},{1,13},{5,17},{9,21},{13,25},... | collective-permute-start | bytes 147464 | tf_op jit(solution)/shard_map/ppermute | solution.py:10
  156.9 1.3 collective-permute-start.7
  158.3 4.7 %collective-permute-done.6 = f32[3,32,128]{2,0,1:T(4,128)S(1)} collective-permute-done((f32[3,32,128]{2,0,1:T(4,128)S(1)}, f32[3,32,128]{2,0,1:T(4,128)S(1)}, u32[]{:S(2)}, u32[]{:S(2)}) %collective-permute-start.6) | collective-permute-done | bytes 49184 | tf_op jit(solution)/shard_map/ppermute | solution.py:10
  163.0 0.9 collective-permute-done.7
  163.9 8.8 %scatter_fusion = f32[3,1025,128]{2,0,1:T(4,128)S(1)} fusion(f32[3,1025,128]{2,0,1:T(4,128)S(1)} %get-tuple-element.29, s32[256]{0:T(256)S(1)} %bitcast.95, f32[256,3,128]{2,1,0:T(4,128)S(1)} %bitcast.91), kind=kCustom, calls=%fused_computation.2 | custom fusion | flops 98304 | bytes 1180672 | tf_op jit(solution)/shard_map/scatter-add | solution.py:61
  173.5 1.9 %collective-permute-start.9 = (f32[3,128,128]{2,0,1:T(4,128)S(1)}, f32[3,128,128]{2,0,1:T(4,128)S(1)}, u32[]{:S(2)}, u32[]{:S(2)}) collective-permute-start(f32[3,128,128]{2,0,1:T(4,128)S(1)} %bitcast.94), channel_id=1, source_target_pairs={{0,1},{1,2},{2,3},{4,5},{5,6},{6,7},{8,9},{9,10},{10,11},{12,13},{... | collective-permute-start | bytes 589832 | tf_op jit(solution)/shard_map/ppermute | solution.py:10
  175.4 5.7 %collective-permute-done.9 = f32[3,128,128]{2,0,1:T(4,128)S(1)} collective-permute-done((f32[3,128,128]{2,0,1:T(4,128)S(1)}, f32[3,128,128]{2,0,1:T(4,128)S(1)}, u32[]{:S(2)}, u32[]{:S(2)}) %collective-permute-start.9) | collective-permute-done | bytes 196640 | tf_op jit(solution)/shard_map/ppermute | solution.py:10
  181.2 2.4 %scatter_fusion.1 = f32[3,1025,128]{2,0,1:T(4,128)S(1)} fusion(f32[3,1025,128]{2,0,1:T(4,128)S(1)} %scatter_fusion, s32[64]{0:T(128)S(1)} %fusion.16, f32[64,3,128]{2,1,0:T(4,128)S(1)} %fusion.15), kind=kCustom, calls=%fused_computation.3 | custom fusion | bytes 295168 | tf_op jit(solution)/shard_map/scatter | solution.py:67
  184.0 1.2 copy.34
  (51 shorter events, 4.3 us)
Async XLA Ops:
  0.6 95.0 %collective-permute-start.8 = (s32[1,64,2]{1,2,0:T(2,128)}, s32[1,64,2]{1,2,0:T(2,128)S(1)}, u32[]{:S(2)}, u32[]{:S(2)}) collective-permute-start(s32[1,64,2]{1,2,0:T(2,128)} %param.21), channel_id=1, source_target_pairs={{1,0},{2,1},{3,2},{5,4},{6,5},{7,6},{9,8},{10,9},{11,10},{13,12},{... | collective-permute-start | bytes 1544 | tf_op jit(solution)/shard_map/ppermute | solution.py:10
  2.6 5.1 %copy-start = (bf16[3072,384]{1,0:T(8,128)(2,1)S(1)}, bf16[3072,384]{1,0:T(8,128)(2,1)}, u32[]{:S(2)}) copy-start(bf16[3072,384]{1,0:T(8,128)(2,1)} %param.12) | copy-start | bytes 7077892
  2.6 5.1 %copy-start.3 = (bf16[384,384]{1,0:T(8,128)(2,1)S(1)}, bf16[384,384]{1,0:T(8,128)(2,1)}, u32[]{:S(2)}) copy-start(bf16[384,384]{1,0:T(8,128)(2,1)} %param.14) | copy-start | bytes 884740
  2.6 5.1 %copy-start.4 = (bf16[384,384]{1,0:T(8,128)(2,1)S(1)}, bf16[384,384]{1,0:T(8,128)(2,1)}, u32[]{:S(2)}) copy-start(bf16[384,384]{1,0:T(8,128)(2,1)} %param.13) | copy-start | bytes 884740
  7.7 2.7 %copy-start.1 = (bf16[3072,384]{0,1:T(8,128)(2,1)S(1)}, bf16[3072,384]{0,1:T(8,128)(2,1)}, u32[]{:S(2)}) copy-start(bf16[3072,384]{0,1:T(8,128)(2,1)} %copy.33) | copy-start | bytes 7077892
  7.7 2.7 %copy-start.6 = (f32[3072]{0:T(1024)S(1)}, f32[3072]{0:T(1024)}, u32[]{:S(2)}) copy-start(f32[3072]{0:T(1024)} %param.16) | copy-start | bytes 36868
  7.7 2.7 %copy-start.7 = (f32[3072]{0:T(1024)S(1)}, f32[3072]{0:T(1024)}, u32[]{:S(2)}) copy-start(f32[3072]{0:T(1024)} %param.15) | copy-start | bytes 36868
  14.9 6.2 %copy-start.2 = (f32[3,1025,128]{2,0,1:T(4,128)S(1)}, f32[3,1025,128]{2,0,1:T(4,128)}, u32[]{:S(2)}) copy-start(f32[3,1025,128]{2,0,1:T(4,128)} %custom-call.5) | copy-start | bytes 4723204
  21.1 73.7 %copy-start.5 = (s32[1,8,32]{2,1,0:T(8,128)S(1)}, s32[1,8,32]{2,1,0:T(8,128)}, u32[]{:S(2)}) copy-start(s32[1,8,32]{2,1,0:T(8,128)} %param.19) | copy-start | bytes 3076
  94.8 80.6 %copy-start.8 = (s32[1,64]{1,0:T(1,128)S(1)}, s32[1,64]{1,0:T(1,128)}, u32[]{:S(2)}) copy-start(s32[1,64]{1,0:T(1,128)} %param.20) | copy-start | bytes 772
  97.0 53.8 %collective-permute-start = (f32[3,32,128]{2,0,1:T(4,128)S(1)}, f32[3,32,128]{2,0,1:T(4,128)S(1)}, u32[]{:S(2)}, u32[]{:S(2)}) collective-permute-start(f32[3,32,128]{2,0,1:T(4,128)S(1)} %get-tuple-element.61), channel_id=1, source_target_pairs={{4,0},{8,4},{12,8},{16,12},{20,16},{24,20},{28,24},{5,1},{9,5},{13... | collective-permute-start | bytes 147464 | tf_op jit(solution)/shard_map/ppermute | solution.py:10
  141.1 13.8 %collective-permute-start.1 = (f32[3,32,128]{2,0,1:T(4,128)S(1)}, f32[3,32,128]{2,0,1:T(4,128)S(1)}, u32[]{:S(2)}, u32[]{:S(2)}) collective-permute-start(f32[3,32,128]{2,0,1:T(4,128)S(1)} %get-tuple-element.60), channel_id=1, source_target_pairs={{8,0},{12,4},{16,8},{20,12},{24,16},{28,20},{9,1},{13,5},{17,9},{2... | collective-permute-start | bytes 147464 | tf_op jit(solution)/shard_map/ppermute | solution.py:10
  143.7 13.2 %collective-permute-start.2 = (f32[3,32,128]{2,0,1:T(4,128)S(1)}, f32[3,32,128]{2,0,1:T(4,128)S(1)}, u32[]{:S(2)}, u32[]{:S(2)}) collective-permute-start(f32[3,32,128]{2,0,1:T(4,128)S(1)} %get-tuple-element.59), channel_id=1, source_target_pairs={{12,0},{16,4},{20,8},{24,12},{28,16},{13,1},{17,5},{21,9},{25,13},... | collective-permute-start | bytes 147464 | tf_op jit(solution)/shard_map/ppermute | solution.py:10
  145.9 12.3 %collective-permute-start.3 = (f32[3,32,128]{2,0,1:T(4,128)S(1)}, f32[3,32,128]{2,0,1:T(4,128)S(1)}, u32[]{:S(2)}, u32[]{:S(2)}) collective-permute-start(f32[3,32,128]{2,0,1:T(4,128)S(1)} %get-tuple-element.58), channel_id=1, source_target_pairs={{16,0},{20,4},{24,8},{28,12},{17,1},{21,5},{25,9},{29,13},{18,2},{... | collective-permute-start | bytes 147464 | tf_op jit(solution)/shard_map/ppermute | solution.py:10
  147.2 11.0 %collective-permute-start.4 = (f32[3,32,128]{2,0,1:T(4,128)S(1)}, f32[3,32,128]{2,0,1:T(4,128)S(1)}, u32[]{:S(2)}, u32[]{:S(2)}) collective-permute-start(f32[3,32,128]{2,0,1:T(4,128)S(1)} %get-tuple-element.57), channel_id=1, source_target_pairs={{0,4},{4,8},{8,12},{12,16},{16,20},{20,24},{24,28},{1,5},{5,9},{9,... | collective-permute-start | bytes 147464 | tf_op jit(solution)/shard_map/ppermute | solution.py:10
  150.8 7.5 %collective-permute-start.5 = (f32[3,32,128]{2,0,1:T(4,128)S(1)}, f32[3,32,128]{2,0,1:T(4,128)S(1)}, u32[]{:S(2)}, u32[]{:S(2)}) collective-permute-start(f32[3,32,128]{2,0,1:T(4,128)S(1)} %get-tuple-element.56), channel_id=1, source_target_pairs={{0,8},{4,12},{8,16},{12,20},{16,24},{20,28},{1,9},{5,13},{9,17},{1... | collective-permute-start | bytes 147464 | tf_op jit(solution)/shard_map/ppermute | solution.py:10
  154.9 8.1 %collective-permute-start.6 = (f32[3,32,128]{2,0,1:T(4,128)S(1)}, f32[3,32,128]{2,0,1:T(4,128)S(1)}, u32[]{:S(2)}, u32[]{:S(2)}) collective-permute-start(f32[3,32,128]{2,0,1:T(4,128)S(1)} %get-tuple-element.55), channel_id=1, source_target_pairs={{0,12},{4,16},{8,20},{12,24},{16,28},{1,13},{5,17},{9,21},{13,25},... | collective-permute-start | bytes 147464 | tf_op jit(solution)/shard_map/ppermute | solution.py:10
  156.9 7.1 %collective-permute-start.7 = (f32[3,32,128]{2,0,1:T(4,128)S(1)}, f32[3,32,128]{2,0,1:T(4,128)S(1)}, u32[]{:S(2)}, u32[]{:S(2)}) collective-permute-start(f32[3,32,128]{2,0,1:T(4,128)S(1)} %get-tuple-element.54), channel_id=1, source_target_pairs={{0,16},{4,20},{8,24},{12,28},{1,17},{5,21},{9,25},{13,29},{2,18},{... | collective-permute-start | bytes 147464 | tf_op jit(solution)/shard_map/ppermute | solution.py:10
  173.5 7.7 %collective-permute-start.9 = (f32[3,128,128]{2,0,1:T(4,128)S(1)}, f32[3,128,128]{2,0,1:T(4,128)S(1)}, u32[]{:S(2)}, u32[]{:S(2)}) collective-permute-start(f32[3,128,128]{2,0,1:T(4,128)S(1)} %bitcast.94), channel_id=1, source_target_pairs={{0,1},{1,2},{2,3},{4,5},{5,6},{6,7},{8,9},{9,10},{10,11},{12,13},{... | collective-permute-start | bytes 589832 | tf_op jit(solution)/shard_map/ppermute | solution.py:10
where the time goes:
time: 187 us; the launch traced here: 186 us
  local copies, waits for them, and re-layouts  69.1 us (37%)
  blocking collectives  40.1 us (21%)
  matrix products  24.2 us (13%)
  starting transfers between devices  24.1 us (13%)
  other arithmetic  13.3 us (7%)
  waiting for transfers between devices  11.4 us (6%)
  between operations  4.13 us (2%)
    dynamic_update_slice x6, local copies, waits for them, and re-layouts, shards(): local_blocks = lax.map(sum_blocks, (elem_block, component_forces))  49.6 us
    psum x1, blocking collectives, shards(): energy = lax.psum(energy_part, ('dom', 'level')) / scale_total  40.1 us
    ppermute x10, starting transfers between devices, from_behind(): return lax.ppermute(block, axis, route)  24.1 us
    dot_general x3, matrix products, sum_blocks(): jnp.dot(selector, component_part, precision=lax.Precision.HIGHEST, prefer...  21.6 us
    ppermute x10, waiting for transfers between devices, from_behind(): return lax.ppermute(block, axis, route)  11.4 us
    scatter-add x1, other arithmetic, shards(): assembled = local_blocks.at[:, slot_blocks.reshape(-1), :].add(received)  8.77 us
    reshape x1, local copies, waits for them, and re-layouts, shards(): forces.reshape(elements, 3, block_size)  6.19 us
    unnamed x27, local copies, waits for them, and re-layouts  5.85 us
  transfers between devices with their start and end apart: 10, of which 3 were waited for; matrix products, arithmetic and copies ran while one was open for 49% of the time, Pallas kernels for 0%

commit v1 on v0

--- a/solution.py
+++ b/solution.py
@@ -66,7 +66,7 @@
     child_values = 0.5 * (parent_pairs[:, :, 0] + parent_pairs[:, :, 1])
     projected = assembled.at[:, hang_child[0], :].set(child_values)
     scale_total = jnp.float32(row_width * elements * lax.axis_size("dom") * lax.axis_size("level"))
-    energy = lax.psum(energy_part, ("dom", "level")) / scale_total
+    energy = lax.psum(lax.psum(energy_part, "level"), "dom") / scale_total
     return (projected[:, :block_count], energy)
 
 

time: 187 us -> 174 us (0.930)
  blocking collectives: 40.1 us -> 22.6 us
  starting transfers between devices: 24.1 us -> 28.7 us
    psum x1 -> x2, blocking collectives: 40.1 us -> 22.6 us  [shards(): energy = lax.psum(lax.psum(energy_part, 'level'), 'dom') / scale_total]
    ppermute x10, starting transfers between devices: 24.1 us -> 28.7 us  [from_behind(): return lax.ppermute(block, axis, route)]
  transfers between devices with their start and end apart: 10 -> 10, of which waited for: 3 -> 3; matrix products, arithmetic and copies ran while one was open for 49% -> 53% of each run, Pallas kernels for 0% -> 0%
where the time goes in v1:
time: 174 us
  local copies, waits for them, and re-layouts  69.1 us (40%)
  starting transfers between devices  28.7 us (16%)
  matrix products  24.2 us (14%)
  blocking collectives  22.6 us (13%)
  other arithmetic  13.3 us (8%)
  waiting for transfers between devices  11.4 us (7%)
  between operations  4.12 us (2%)
    dynamic_update_slice x6, local copies, waits for them, and re-layouts, shards(): local_blocks = lax.map(sum_blocks, (elem_block, component_forces))  49.6 us
    ppermute x10, starting transfers between devices, from_behind(): return lax.ppermute(block, axis, route)  28.7 us
    psum x2, blocking collectives, shards(): energy = lax.psum(lax.psum(energy_part, 'level'), 'dom') / scale_total  22.6 us
    dot_general x3, matrix products, sum_blocks(): jnp.dot(selector, component_part, precision=lax.Precision.HIGHEST, prefer...  21.6 us
    ppermute x10, waiting for transfers between devices, from_behind(): return lax.ppermute(block, axis, route)  11.4 us
    scatter-add x1, other arithmetic, shards(): assembled = local_blocks.at[:, slot_blocks.reshape(-1), :].add(received)  8.77 us
    reshape x1, local copies, waits for them, and re-layouts, shards(): forces.reshape(elements, 3, block_size)  6.2 us
    unnamed x27, local copies, waits for them, and re-layouts  5.85 us
  transfers between devices with their start and end apart: 10, of which 3 were waited for; matrix products, arithmetic and copies ran while one was open for 53% of the time, Pallas kernels for 0%

profile of v1, /device:TPU:18, one launch (start us, length us, event | category | flops | bytes accessed | tf_op | source)
XLA Modules:
  0.0 173.5 jit_solution(3185684533033974537)
XLA Ops:
  0.6 1.9 %collective-permute-start.8 = (s32[1,64,2]{1,2,0:T(2,128)}, s32[1,64,2]{1,2,0:T(2,128)S(1)}, u32[]{:S(2)}, u32[]{:S(2)}) collective-permute-start(s32[1,64,2]{1,2,0:T(2,128)} %param.21), channel_id=1, source_target_pairs={{1,0},{2,1},{3,2},{5,4},{6,5},{7,6},{9,8},{10,9},{11,10},{13,12},{... | collective-permute-start | bytes 1544 | tf_op jit(solution)/shard_map/ppermute | solution.py:10
  2.6 4.4 %copy.33 = bf16[3072,384]{0,1:T(8,128)(2,1)} copy(bf16[3072,384]{1,0:T(8,128)(2,1)} %param.12) | data formatting | bytes 4718592 | tf_op args[0]
  7.8 2.7 %convolution_bitcast_fusion = f32[3072,768]{0,1:T(8,128)S(1)} fusion(bf16[3072,384]{1,0:T(8,128)(2,1)S(1)} %copy-done, bf16[384,384]{1,0:T(8,128)(2,1)S(1)} %copy-done.3, bf16[384,384]{1,0:T(8,128)(2,1)S(1)} %copy-done.4), kind=kOutput, calls=%fused_computation.13 | convolution fusion | flops 1813118976 | bytes 12386304 | tf_op jit(solution)/shard_map/dot_general | solution.py:31
  10.4 4.5 %multiply_reduce_fusion = (f32[]{:T(128)}, f32[3072,384]{0,1:T(8,128)}) fusion(bf16[3072,384]{0,1:T(8,128)(2,1)S(1)} %copy-done.1, f32[3072,768]{0,1:T(8,128)S(1)} %convolution_bitcast_fusion, f32[3072]{0:T(1024)S(1)} %copy-done.6, f32[3072]{0:T(1024)S(1)} %copy-done.7, pred[3072]{0:T(1024)(128)(4,1)S(1)} %iota_compare_fusion.4), kind=kLoop, calls=%fused_computation.18 | loop fusion | flops 8257535 | bytes 16542724 | tf_op jit(solution)/shard_map/reduce_sum | solution.py:35
  14.9 6.2 %copy.27 = f32[3072,3,128]{2,0,1:T(8,128)} copy(f32[3072,3,128]{0,2,1:T(8,128)} %bitcast.88) | data formatting | bytes 9437184 | tf_op jit(solution)/shard_map/reshape | solution.py:36
  21.1 73.7 %while.11 = (s32[]{:T(128)}, f32[3,1025,128]{2,0,1:T(4,128)S(1)}, s32[3,3072]{1,0:T(4,128)}, f32[3,3072,128]{2,1,0:T(8,128)}, s32[]{:T(128)}, /*index=5*/s32[]{:T(128)}) while((s32[]{:T(128)}, f32[3,1025,128]{2,0,1:T(4,128)S(1)}, s32[3,3072]{1,0:T(4,128)}, f32[3,3072,128]{2,1,0:T(8,128)}, s32[]{:T(128)}, /*index=5*/s32[]{:T(128)}) %tuple.40), condition=%wide.region_1.2_spmd.clone, body=%wide.region_0.1_spmd.clone.sunk | while | flops 4839705600 | bytes 4234317 | solution.py:49
  21.9 7.2 %fusion.24 = f32[1,1025,128]{2,1,0:T(8,128)S(1)} fusion(s32[3072]{0:T(1024)S(1)} %bitcast.92, f32[3,3072,128]{2,1,0:T(8,128)} %get-tuple-element.104, s32[]{:T(128)} %get-tuple-element.95), kind=kOutput, calls=%fused_computation.8.clone.1 | convolution fusion | flops 4839705600 | bytes 2110464 | tf_op jit(solution)/shard_map/while/body/eval_jaxpr/dot_general | solution.py:42
  29.1 3.3 %copy.41 = f32[1,1025,128]{2,0,1:T(1,128)S(1)} copy(f32[1,1025,128]{2,1,0:T(8,128)S(1)} %fusion.24) | data formatting | bytes 1049600 | tf_op jit(solution)/shard_map/while/body/jit(dynamic_update_index_in_dim)/dynamic_update_slice | solution.py:49
  32.4 13.2 %dynamic_update_slice.6 = f32[3,1025,128]{2,0,1:T(4,128)S(1)} dynamic-update-slice(f32[3,1025,128]{2,0,1:T(4,128)S(1)} %get-tuple-element.96, f32[1,1025,128]{2,0,1:T(1,128)S(1)} %copy.41, s32[]{:T(128)} %get-tuple-element.95, s32[]{:T(128)} %constant.11.clone.1..sunk, s32[]{:T(128)} %constant.11.clone.1..sunk) | dynamic-update-slice | bytes 1049604 | tf_op jit(solution)/shard_map/while/body/jit(dynamic_update_index_in_dim)/dynamic_update_slice | solution.py:49
  46.5 7.2 %fusion.24 = f32[1,1025,128]{2,1,0:T(8,128)S(1)} fusion(s32[3072]{0:T(1024)S(1)} %bitcast.92, f32[3,3072,128]{2,1,0:T(8,128)} %get-tuple-element.104, s32[]{:T(128)} %get-tuple-element.95), kind=kOutput, calls=%fused_computation.8.clone.1 | convolution fusion | flops 4839705600 | bytes 2110464 | tf_op jit(solution)/shard_map/while/body/eval_jaxpr/dot_general | solution.py:42
  53.7 3.3 %copy.41 = f32[1,1025,128]{2,0,1:T(1,128)S(1)} copy(f32[1,1025,128]{2,1,0:T(8,128)S(1)} %fusion.24) | data formatting | bytes 1049600 | tf_op jit(solution)/shard_map/while/body/jit(dynamic_update_index_in_dim)/dynamic_update_slice | solution.py:49
  57.0 13.2 %dynamic_update_slice.6 = f32[3,1025,128]{2,0,1:T(4,128)S(1)} dynamic-update-slice(f32[3,1025,128]{2,0,1:T(4,128)S(1)} %get-tuple-element.96, f32[1,1025,128]{2,0,1:T(1,128)S(1)} %copy.41, s32[]{:T(128)} %get-tuple-element.95, s32[]{:T(128)} %constant.11.clone.1..sunk, s32[]{:T(128)} %constant.11.clone.1..sunk) | dynamic-update-slice | bytes 1049604 | tf_op jit(solution)/shard_map/while/body/jit(dynamic_update_index_in_dim)/dynamic_update_slice | solution.py:49
  71.1 7.2 %fusion.24 = f32[1,1025,128]{2,1,0:T(8,128)S(1)} fusion(s32[3072]{0:T(1024)S(1)} %bitcast.92, f32[3,3072,128]{2,1,0:T(8,128)} %get-tuple-element.104, s32[]{:T(128)} %get-tuple-element.95), kind=kOutput, calls=%fused_computation.8.clone.1 | convolution fusion | flops 4839705600 | bytes 2110464 | tf_op jit(solution)/shard_map/while/body/eval_jaxpr/dot_general | solution.py:42
  78.2 3.3 %copy.41 = f32[1,1025,128]{2,0,1:T(1,128)S(1)} copy(f32[1,1025,128]{2,1,0:T(8,128)S(1)} %fusion.24) | data formatting | bytes 1049600 | tf_op jit(solution)/shard_map/while/body/jit(dynamic_update_index_in_dim)/dynamic_update_slice | solution.py:49
  81.5 13.2 %dynamic_update_slice.6 = f32[3,1025,128]{2,0,1:T(4,128)S(1)} dynamic-update-slice(f32[3,1025,128]{2,0,1:T(4,128)S(1)} %get-tuple-element.96, f32[1,1025,128]{2,0,1:T(1,128)S(1)} %copy.41, s32[]{:T(128)} %get-tuple-element.95, s32[]{:T(128)} %constant.11.clone.1..sunk, s32[]{:T(128)} %constant.11.clone.1..sunk) | dynamic-update-slice | bytes 1049604 | tf_op jit(solution)/shard_map/while/body/jit(dynamic_update_index_in_dim)/dynamic_update_slice | solution.py:49
  95.5 6.8 %psum.14 = f32[]{:T(128)} all-reduce(f32[]{:T(128)S(6)} %mul.39), channel_id=1, replica_groups=mesh['dom'=8,'level'=4] {'level'}, use_global_device_ids=true, to_apply=%region_5.6 | all-reduce | flops 1 | bytes 8 | tf_op jit(solution)/shard_map/psum | solution.py:69
  103.8 3.3 %collective-permute-start = (f32[3,32,128]{2,0,1:T(4,128)S(1)}, f32[3,32,128]{2,0,1:T(4,128)S(1)}, u32[]{:S(2)}, u32[]{:S(2)}) collective-permute-start(f32[3,32,128]{2,0,1:T(4,128)S(1)} %get-tuple-element.61), channel_id=1, source_target_pairs={{4,0},{8,4},{12,8},{16,12},{20,16},{24,20},{28,24},{5,1},{9,5},{13... | collective-permute-start | bytes 147464 | tf_op jit(solution)/shard_map/ppermute | solution.py:10
  107.1 15.8 %psum.15 = f32[]{:T(128)} all-reduce(f32[]{:T(128)} %psum.14), channel_id=1, replica_groups=mesh['dom'=8,'level'=4] {'dom'}, use_global_device_ids=true, to_apply=%region_6.7 | all-reduce | flops 1 | bytes 8 | tf_op jit(solution)/shard_map/psum | solution.py:69
  123.6 5.2 %collective-permute-start.1 = (f32[3,32,128]{2,0,1:T(4,128)S(1)}, f32[3,32,128]{2,0,1:T(4,128)S(1)}, u32[]{:S(2)}, u32[]{:S(2)}) collective-permute-start(f32[3,32,128]{2,0,1:T(4,128)S(1)} %get-tuple-element.60), channel_id=1, source_target_pairs={{8,0},{12,4},{16,8},{20,12},{24,16},{28,20},{9,1},{13,5},{17,9},{2... | collective-permute-start | bytes 147464 | tf_op jit(solution)/shard_map/ppermute | solution.py:10
  128.8 2.1 %collective-permute-start.2 = (f32[3,32,128]{2,0,1:T(4,128)S(1)}, f32[3,32,128]{2,0,1:T(4,128)S(1)}, u32[]{:S(2)}, u32[]{:S(2)}) collective-permute-start(f32[3,32,128]{2,0,1:T(4,128)S(1)} %get-tuple-element.59), channel_id=1, source_target_pairs={{12,0},{16,4},{20,8},{24,12},{28,16},{13,1},{17,5},{21,9},{25,13},... | collective-permute-start | bytes 147464 | tf_op jit(solution)/shard_map/ppermute | solution.py:10
  130.9 3.1 %collective-permute-start.3 = (f32[3,32,128]{2,0,1:T(4,128)S(1)}, f32[3,32,128]{2,0,1:T(4,128)S(1)}, u32[]{:S(2)}, u32[]{:S(2)}) collective-permute-start(f32[3,32,128]{2,0,1:T(4,128)S(1)} %get-tuple-element.58), channel_id=1, source_target_pairs={{16,0},{20,4},{24,8},{28,12},{17,1},{21,5},{25,9},{29,13},{18,2},{... | collective-permute-start | bytes 147464 | tf_op jit(solution)/shard_map/ppermute | solution.py:10
  134.1 4.6 %collective-permute-start.4 = (f32[3,32,128]{2,0,1:T(4,128)S(1)}, f32[3,32,128]{2,0,1:T(4,128)S(1)}, u32[]{:S(2)}, u32[]{:S(2)}) collective-permute-start(f32[3,32,128]{2,0,1:T(4,128)S(1)} %get-tuple-element.57), channel_id=1, source_target_pairs={{0,4},{4,8},{8,12},{12,16},{16,20},{20,24},{24,28},{1,5},{5,9},{9,... | collective-permute-start | bytes 147464 | tf_op jit(solution)/shard_map/ppermute | solution.py:10
  138.6 3.4 %collective-permute-start.5 = (f32[3,32,128]{2,0,1:T(4,128)S(1)}, f32[3,32,128]{2,0,1:T(4,128)S(1)}, u32[]{:S(2)}, u32[]{:S(2)}) collective-permute-start(f32[3,32,128]{2,0,1:T(4,128)S(1)} %get-tuple-element.56), channel_id=1, source_target_pairs={{0,8},{4,12},{8,16},{12,20},{16,24},{20,28},{1,9},{5,13},{9,17},{1... | collective-permute-start | bytes 147464 | tf_op jit(solution)/shard_map/ppermute | solution.py:10
  142.0 1.9 %collective-permute-start.6 = (f32[3,32,128]{2,0,1:T(4,128)S(1)}, f32[3,32,128]{2,0,1:T(4,128)S(1)}, u32[]{:S(2)}, u32[]{:S(2)}) collective-permute-start(f32[3,32,128]{2,0,1:T(4,128)S(1)} %get-tuple-element.55), channel_id=1, source_target_pairs={{0,12},{4,16},{8,20},{12,24},{16,28},{1,13},{5,17},{9,21},{13,25},... | collective-permute-start | bytes 147464 | tf_op jit(solution)/shard_map/ppermute | solution.py:10
  144.0 1.3 collective-permute-start.7
  145.4 4.6 %collective-permute-done.6 = f32[3,32,128]{2,0,1:T(4,128)S(1)} collective-permute-done((f32[3,32,128]{2,0,1:T(4,128)S(1)}, f32[3,32,128]{2,0,1:T(4,128)S(1)}, u32[]{:S(2)}, u32[]{:S(2)}) %collective-permute-start.6) | collective-permute-done | bytes 49184 | tf_op jit(solution)/shard_map/ppermute | solution.py:10
  150.0 1.0 collective-permute-done.7
  151.1 8.8 %scatter_fusion = f32[3,1025,128]{2,0,1:T(4,128)S(1)} fusion(f32[3,1025,128]{2,0,1:T(4,128)S(1)} %get-tuple-element.29, s32[256]{0:T(256)S(1)} %bitcast.95, f32[256,3,128]{2,1,0:T(4,128)S(1)} %bitcast.91), kind=kCustom, calls=%fused_computation.2 | custom fusion | flops 98304 | bytes 1180672 | tf_op jit(solution)/shard_map/scatter-add | solution.py:61
  160.6 1.9 %collective-permute-start.9 = (f32[3,128,128]{2,0,1:T(4,128)S(1)}, f32[3,128,128]{2,0,1:T(4,128)S(1)}, u32[]{:S(2)}, u32[]{:S(2)}) collective-permute-start(f32[3,128,128]{2,0,1:T(4,128)S(1)} %bitcast.94), channel_id=1, source_target_pairs={{0,1},{1,2},{2,3},{4,5},{5,6},{6,7},{8,9},{9,10},{10,11},{12,13},{... | collective-permute-start | bytes 589832 | tf_op jit(solution)/shard_map/ppermute | solution.py:10
  162.6 5.7 %collective-permute-done.9 = f32[3,128,128]{2,0,1:T(4,128)S(1)} collective-permute-done((f32[3,128,128]{2,0,1:T(4,128)S(1)}, f32[3,128,128]{2,0,1:T(4,128)S(1)}, u32[]{:S(2)}, u32[]{:S(2)}) %collective-permute-start.9) | collective-permute-done | bytes 196640 | tf_op jit(solution)/shard_map/ppermute | solution.py:10
  168.4 2.4 %scatter_fusion.1 = f32[3,1025,128]{2,0,1:T(4,128)S(1)} fusion(f32[3,1025,128]{2,0,1:T(4,128)S(1)} %scatter_fusion, s32[64]{0:T(128)S(1)} %fusion.16, f32[64,3,128]{2,1,0:T(4,128)S(1)} %fusion.15), kind=kCustom, calls=%fused_computation.3 | custom fusion | bytes 295168 | tf_op jit(solution)/shard_map/scatter | solution.py:67
  171.2 1.2 copy.34
  (52 shorter events, 5.3 us)
Async XLA Ops:
  0.6 101.8 %collective-permute-start.8 = (s32[1,64,2]{1,2,0:T(2,128)}, s32[1,64,2]{1,2,0:T(2,128)S(1)}, u32[]{:S(2)}, u32[]{:S(2)}) collective-permute-start(s32[1,64,2]{1,2,0:T(2,128)} %param.21), channel_id=1, source_target_pairs={{1,0},{2,1},{3,2},{5,4},{6,5},{7,6},{9,8},{10,9},{11,10},{13,12},{... | collective-permute-start | bytes 1544 | tf_op jit(solution)/shard_map/ppermute | solution.py:10
  2.6 5.1 %copy-start = (bf16[3072,384]{1,0:T(8,128)(2,1)S(1)}, bf16[3072,384]{1,0:T(8,128)(2,1)}, u32[]{:S(2)}) copy-start(bf16[3072,384]{1,0:T(8,128)(2,1)} %param.12) | copy-start | bytes 7077892
  2.6 5.1 %copy-start.3 = (bf16[384,384]{1,0:T(8,128)(2,1)S(1)}, bf16[384,384]{1,0:T(8,128)(2,1)}, u32[]{:S(2)}) copy-start(bf16[384,384]{1,0:T(8,128)(2,1)} %param.14) | copy-start | bytes 884740
  2.6 5.1 %copy-start.4 = (bf16[384,384]{1,0:T(8,128)(2,1)S(1)}, bf16[384,384]{1,0:T(8,128)(2,1)}, u32[]{:S(2)}) copy-start(bf16[384,384]{1,0:T(8,128)(2,1)} %param.13) | copy-start | bytes 884740
  7.7 2.7 %copy-start.1 = (bf16[3072,384]{0,1:T(8,128)(2,1)S(1)}, bf16[3072,384]{0,1:T(8,128)(2,1)}, u32[]{:S(2)}) copy-start(bf16[3072,384]{0,1:T(8,128)(2,1)} %copy.33) | copy-start | bytes 7077892
  7.7 2.7 %copy-start.6 = (f32[3072]{0:T(1024)S(1)}, f32[3072]{0:T(1024)}, u32[]{:S(2)}) copy-start(f32[3072]{0:T(1024)} %param.16) | copy-start | bytes 36868
  7.7 2.7 %copy-start.7 = (f32[3072]{0:T(1024)S(1)}, f32[3072]{0:T(1024)}, u32[]{:S(2)}) copy-start(f32[3072]{0:T(1024)} %param.15) | copy-start | bytes 36868
  14.9 6.2 %copy-start.2 = (f32[3,1025,128]{2,0,1:T(4,128)S(1)}, f32[3,1025,128]{2,0,1:T(4,128)}, u32[]{:S(2)}) copy-start(f32[3,1025,128]{2,0,1:T(4,128)} %custom-call.5) | copy-start | bytes 4723204
  21.1 74.4 %copy-start.5 = (s32[1,8,32]{2,1,0:T(8,128)S(1)}, s32[1,8,32]{2,1,0:T(8,128)}, u32[]{:S(2)}) copy-start(s32[1,8,32]{2,1,0:T(8,128)} %param.19) | copy-start | bytes 3076
  94.8 67.8 %copy-start.8 = (s32[1,64]{1,0:T(1,128)S(1)}, s32[1,64]{1,0:T(1,128)}, u32[]{:S(2)}) copy-start(s32[1,64]{1,0:T(1,128)} %param.20) | copy-start | bytes 772
  103.8 34.8 %collective-permute-start = (f32[3,32,128]{2,0,1:T(4,128)S(1)}, f32[3,32,128]{2,0,1:T(4,128)S(1)}, u32[]{:S(2)}, u32[]{:S(2)}) collective-permute-start(f32[3,32,128]{2,0,1:T(4,128)S(1)} %get-tuple-element.61), channel_id=1, source_target_pairs={{4,0},{8,4},{12,8},{16,12},{20,16},{24,20},{28,24},{5,1},{9,5},{13... | collective-permute-start | bytes 147464 | tf_op jit(solution)/shard_map/ppermute | solution.py:10
  123.6 18.4 %collective-permute-start.1 = (f32[3,32,128]{2,0,1:T(4,128)S(1)}, f32[3,32,128]{2,0,1:T(4,128)S(1)}, u32[]{:S(2)}, u32[]{:S(2)}) collective-permute-start(f32[3,32,128]{2,0,1:T(4,128)S(1)} %get-tuple-element.60), channel_id=1, source_target_pairs={{8,0},{12,4},{16,8},{20,12},{24,16},{28,20},{9,1},{13,5},{17,9},{2... | collective-permute-start | bytes 147464 | tf_op jit(solution)/shard_map/ppermute | solution.py:10
  128.8 15.2 %collective-permute-start.2 = (f32[3,32,128]{2,0,1:T(4,128)S(1)}, f32[3,32,128]{2,0,1:T(4,128)S(1)}, u32[]{:S(2)}, u32[]{:S(2)}) collective-permute-start(f32[3,32,128]{2,0,1:T(4,128)S(1)} %get-tuple-element.59), channel_id=1, source_target_pairs={{12,0},{16,4},{20,8},{24,12},{28,16},{13,1},{17,5},{21,9},{25,13},... | collective-permute-start | bytes 147464 | tf_op jit(solution)/shard_map/ppermute | solution.py:10
  130.9 14.4 %collective-permute-start.3 = (f32[3,32,128]{2,0,1:T(4,128)S(1)}, f32[3,32,128]{2,0,1:T(4,128)S(1)}, u32[]{:S(2)}, u32[]{:S(2)}) collective-permute-start(f32[3,32,128]{2,0,1:T(4,128)S(1)} %get-tuple-element.58), channel_id=1, source_target_pairs={{16,0},{20,4},{24,8},{28,12},{17,1},{21,5},{25,9},{29,13},{18,2},{... | collective-permute-start | bytes 147464 | tf_op jit(solution)/shard_map/ppermute | solution.py:10
  134.1 11.3 %collective-permute-start.4 = (f32[3,32,128]{2,0,1:T(4,128)S(1)}, f32[3,32,128]{2,0,1:T(4,128)S(1)}, u32[]{:S(2)}, u32[]{:S(2)}) collective-permute-start(f32[3,32,128]{2,0,1:T(4,128)S(1)} %get-tuple-element.57), channel_id=1, source_target_pairs={{0,4},{4,8},{8,12},{12,16},{16,20},{20,24},{24,28},{1,5},{5,9},{9,... | collective-permute-start | bytes 147464 | tf_op jit(solution)/shard_map/ppermute | solution.py:10
  138.6 6.8 %collective-permute-start.5 = (f32[3,32,128]{2,0,1:T(4,128)S(1)}, f32[3,32,128]{2,0,1:T(4,128)S(1)}, u32[]{:S(2)}, u32[]{:S(2)}) collective-permute-start(f32[3,32,128]{2,0,1:T(4,128)S(1)} %get-tuple-element.56), channel_id=1, source_target_pairs={{0,8},{4,12},{8,16},{12,20},{16,24},{20,28},{1,9},{5,13},{9,17},{1... | collective-permute-start | bytes 147464 | tf_op jit(solution)/shard_map/ppermute | solution.py:10
  142.0 8.0 %collective-permute-start.6 = (f32[3,32,128]{2,0,1:T(4,128)S(1)}, f32[3,32,128]{2,0,1:T(4,128)S(1)}, u32[]{:S(2)}, u32[]{:S(2)}) collective-permute-start(f32[3,32,128]{2,0,1:T(4,128)S(1)} %get-tuple-element.55), channel_id=1, source_target_pairs={{0,12},{4,16},{8,20},{12,24},{16,28},{1,13},{5,17},{9,21},{13,25},... | collective-permute-start | bytes 147464 | tf_op jit(solution)/shard_map/ppermute | solution.py:10
  144.0 7.1 %collective-permute-start.7 = (f32[3,32,128]{2,0,1:T(4,128)S(1)}, f32[3,32,128]{2,0,1:T(4,128)S(1)}, u32[]{:S(2)}, u32[]{:S(2)}) collective-permute-start(f32[3,32,128]{2,0,1:T(4,128)S(1)} %get-tuple-element.54), channel_id=1, source_target_pairs={{0,16},{4,20},{8,24},{12,28},{1,17},{5,21},{9,25},{13,29},{2,18},{... | collective-permute-start | bytes 147464 | tf_op jit(solution)/shard_map/ppermute | solution.py:10
  160.6 7.7 %collective-permute-start.9 = (f32[3,128,128]{2,0,1:T(4,128)S(1)}, f32[3,128,128]{2,0,1:T(4,128)S(1)}, u32[]{:S(2)}, u32[]{:S(2)}) collective-permute-start(f32[3,128,128]{2,0,1:T(4,128)S(1)} %bitcast.94), channel_id=1, source_target_pairs={{0,1},{1,2},{2,3},{4,5},{5,6},{6,7},{8,9},{9,10},{10,11},{12,13},{... | collective-permute-start | bytes 589832 | tf_op jit(solution)/shard_map/ppermute | solution.py:10
